TPU v7x, 32 devices: a whole 2x2x4 slice. The times are simulated.
32 devices in a mesh: tile: 8 (over z, x), sub: 4 (over y, core).
Axes of the slice: x: 2, y: 2, z: 4, core: 2. Of those that a mesh axis runs over, the one named last changes fastest.
Arguments:
- grid_feats: bfloat16 [4096, 512], P(('tile', 'sub')), may hold values from -6 to 6
- mesh_feats: bfloat16 [4096, 512], P(('tile', 'sub')), may hold values from -6 to 6
- encode_edges: bfloat16 [32768, 512], P(('tile', 'sub')), may hold values from -6 to 6
- decode_edges: bfloat16 [16384, 512], P(('tile', 'sub')), may hold values from -6 to 6
- encode_source: int32 [32768], P(('tile', 'sub')), may hold values from 0 to 4095, as said below
- encode_target: int32 [32768], P(('tile', 'sub')), may hold values from -1 to 4095, as said below
- decode_source: int32 [16384], P(('tile', 'sub')), may hold values from 0 to 4095, as said below
- decode_target: int32 [16384], P(('tile', 'sub')), may hold values from -1 to 4095, as said below
- owner_fine: int32 [4096], P(('tile', 'sub')), may hold values from 0 to 1023, as said below
- owner_coarse: int32 [1024], P('tile'), may hold values from 0 to 511
- encode_weight: bfloat16 [512, 512], replicated, may hold values from -0.25 to 0.25
- decode_weight: bfloat16 [512, 512], replicated, may hold values from -0.25 to 0.25
- middle_weight: bfloat16 [512, 512], replicated, may hold values from -0.25 to 0.25
- summit_weight: bfloat16 [512, 512], replicated, may hold values from -0.25 to 0.25
- cotangent: bfloat16 [4096, 512], P(('tile', 'sub')), may hold values from -6 to 6
Outputs:
- grid_update: bfloat16 [4096, 512], P(('tile', 'sub'))
- encode_grad: float32 [512, 512], replicated
- decode_grad: float32 [512, 512], replicated
- middle_grad: float32 [512, 512], replicated
- summit_grad: float32 [512, 512], replicated
Inputs may be any that keep to these rules, and one draw needn't show every extreme that they name: `encode_source`: edge slot e is listed on device d = e // 1024; its source grid node lies on device d - 1, d or d + 1. `encode_target`: -1 marks padding; every other value is a mesh node of the device that lists the slot. On each device padding fills whole blocks of 128 slots after all live ones; every device has a live block, and some device has no padding. `decode_source`: edge slot e is listed on device d = e // 512; its source mesh node lies on device d - 1, d or d + 1. `decode_target`: -1 marks padding; every other value is a grid node of the device that lists the slot. On each device padding fills whole blocks of 128 slots after all live ones; every device has a live block, and some device has no padding. `owner_fine`: the middle node of fine mesh node m lies on the tile of the device that holds m.
All inputs are finite; a program needn't handle non-finite values.
Results may differ from a plain program's by a relative error of at most 0.012.
Values may be sent and summed in bfloat16 or wider, within the bound.
No kernel may reach another device: no remote copies, remote signals or barrier semaphores. Data moves between devices by JAX's collectives and lax.ppermute only.
A program may use at most 64 MiB of HBM per device.

v0:
```python
import jax
import jax.numpy as jnp
from jax import lax
from jax.sharding import PartitionSpec as P

TOP_NODES = 512
BLOCK = 128


def extended(x, sides, width):
    for axis, dim in sides:
        peers, length = (lax.axis_size(axis), x.shape[dim])
        up = [(i, (i + 1) % peers) for i in range(peers - 1)]
        down = [(j, i) for i, j in up]
        last = lax.slice_in_dim(x, length - width, length, axis=dim)
        initial = lax.slice_in_dim(x, 0, width, axis=dim)
        before = lax.ppermute(last, axis, up)
        after = lax.ppermute(initial, axis, down)
        x = jnp.concatenate([before, x, after], axis=dim)
    return x


def from_behind(x, axis, by):
    peers = lax.axis_size(axis)
    pairs = [(i, i + by) for i in range(peers) if 0 <= i + by < peers]
    return lax.ppermute(x, axis, pairs)


def silu_slope(values):
    sigmoid = jax.nn.sigmoid(values)
    return sigmoid * (1.0 + values * (1.0 - sigmoid))


def live_count(targets):
    heads = targets.reshape(-1, BLOCK)[:, 0]
    return jnp.sum((heads >= 0).astype(jnp.int32))


def local_targets(targets, first, limit):
    return jnp.where(targets >= 0, targets - first, limit)


def outer_sum(left, right):
    return lax.dot_general(
        left, right, (((0,), (0,)), ((), ())), preferred_element_type=jnp.float32
    )


def times_transposed(left, right):
    return lax.dot_general(
        left, right, (((1,), (1,)), ((), ())), preferred_element_type=jnp.float32
    )


def membership(indices, rows, dtype):
    return (jnp.arange(rows, dtype=jnp.int32)[:, None] == indices[None, :]).astype(dtype)


def exact_sum(members, values):
    return jnp.dot(
        members, values, precision=lax.Precision.HIGHEST, preferred_element_type=jnp.float32
    )


def edge_forward(sources, senders, targets, edge_feats, weight, segments, blocks):
    features = weight.shape[1]

    def block_step(block_id, carried):
        summed, stored = carried
        offset = block_id * BLOCK
        picked = lax.dynamic_slice_in_dim(senders, offset, BLOCK)
        receivers = lax.dynamic_slice_in_dim(targets, offset, BLOCK)
        edge_part = lax.dynamic_slice_in_dim(edge_feats, offset, BLOCK, 0)
        fetched = jnp.take(sources, picked, axis=0)
        preact = jnp.dot(fetched, weight, preferred_element_type=jnp.float32) + edge_part.astype(
            jnp.float32
        )
        summed = summed + exact_sum(
            membership(receivers, segments, jnp.float32), jax.nn.silu(preact)
        )
        stored = lax.dynamic_update_slice_in_dim(stored, preact, offset, 0)
        return (summed, stored)

    start_sum = jnp.zeros((segments, features), jnp.float32)
    start_store = jnp.zeros((senders.shape[0], features), jnp.float32)
    return lax.fori_loop(0, blocks, block_step, (start_sum, start_store))


def edge_backward(
    sources, senders, targets, stored, weight, upstream, factor, blocks, returned_rows
):
    features = weight.shape[1]

    def block_step(block_id, carried):
        gradient, returned = carried
        offset = block_id * BLOCK
        picked = lax.dynamic_slice_in_dim(senders, offset, BLOCK)
        receivers = lax.dynamic_slice_in_dim(targets, offset, BLOCK)
        preact = lax.dynamic_slice_in_dim(stored, offset, BLOCK, 0)
        fetched = jnp.take(sources, picked, axis=0)
        incoming = jnp.take(upstream, receivers, axis=0).astype(jnp.float32) * factor
        slope = (incoming * silu_slope(preact)).astype(jnp.bfloat16)
        gradient = gradient + outer_sum(fetched, slope)
        if returned_rows:
            passed = times_transposed(slope, weight)
            returned = returned + exact_sum(membership(picked, returned_rows, jnp.float32), passed)
        return (gradient, returned)

    start_grad = jnp.zeros((features, features), jnp.float32)
    start_back = jnp.zeros((max(returned_rows, 1), features), jnp.float32)
    return lax.fori_loop(0, blocks, block_step, (start_grad, start_back))


def shards(
    grid_feats,
    mesh_feats,
    encode_edges,
    decode_edges,
    encode_source,
    encode_target,
    decode_source,
    decode_target,
    owner_fine,
    owner_coarse,
    encode_weight,
    decode_weight,
    middle_weight,
    summit_weight,
    cotangent,
):
    grid_rows = grid_feats.shape[0]
    mesh_rows = mesh_feats.shape[0]
    level_rows = owner_coarse.shape[0]
    tiles = lax.axis_size("tile")
    subs = lax.axis_size("sub")
    device = lax.axis_index(("tile", "sub"))
    tile_id = lax.axis_index("tile")
    encode_factor = mesh_rows / encode_source.shape[0]
    decode_factor = grid_rows / decode_source.shape[0]
    middle_factor = level_rows / (mesh_rows * subs)
    summit_factor = TOP_NODES / (level_rows * tiles)
    grid_wide = extended(grid_feats, ((("tile", "sub"), 0),), grid_rows)
    encode_senders = encode_source - (device - 1) * grid_rows
    encode_targets = local_targets(encode_target, device * mesh_rows, mesh_rows)
    encode_blocks = live_count(encode_target)
    encode_summed, encode_stored = edge_forward(
        grid_wide,
        encode_senders,
        encode_targets,
        encode_edges,
        encode_weight,
        mesh_rows,
        encode_blocks,
    )
    mesh_mid = (mesh_feats.astype(jnp.float32) + encode_factor * encode_summed).astype(jnp.bfloat16)
    fine_local = owner_fine - tile_id * level_rows
    fine_members = membership(fine_local, level_rows, jnp.bfloat16)
    middle_part = jnp.dot(fine_members, mesh_mid, preferred_element_type=jnp.float32)
    middle_sum = lax.psum(middle_part, "sub")
    middle_in = (middle_factor * middle_sum).astype(jnp.bfloat16)
    middle_act = jnp.dot(middle_in, middle_weight, preferred_element_type=jnp.float32)
    middle_out = (middle_in.astype(jnp.float32) + jax.nn.silu(middle_act)).astype(jnp.bfloat16)
    top_members = membership(owner_coarse, TOP_NODES, jnp.bfloat16)
    summit_part = jnp.dot(top_members, middle_out, preferred_element_type=jnp.float32)
    summit_whole = lax.psum(summit_part, "tile")
    summit_in = (summit_factor * summit_whole).astype(jnp.bfloat16)
    summit_act = jnp.dot(summit_in, summit_weight, preferred_element_type=jnp.float32)
    summit_out = jax.nn.silu(summit_act).astype(jnp.bfloat16)
    coarse_of = jnp.take(owner_coarse, fine_local)
    lifted = jnp.take(middle_out, fine_local, axis=0).astype(jnp.float32) + jnp.take(
        summit_out, coarse_of, axis=0
    ).astype(jnp.float32)
    mesh_out = (mesh_mid.astype(jnp.float32) + lifted).astype(jnp.bfloat16)
    mesh_wide = extended(mesh_out, ((("tile", "sub"), 0),), mesh_rows)
    decode_senders = decode_source - (device - 1) * mesh_rows
    decode_targets = local_targets(decode_target, device * grid_rows, grid_rows)
    decode_blocks = live_count(decode_target)
    decode_summed, decode_stored = edge_forward(
        mesh_wide,
        decode_senders,
        decode_targets,
        decode_edges,
        decode_weight,
        grid_rows,
        decode_blocks,
    )
    grid_update = (grid_feats.astype(jnp.float32) + decode_factor * decode_summed).astype(
        jnp.bfloat16
    )
    decode_local, decode_returned = edge_backward(
        mesh_wide,
        decode_senders,
        decode_targets,
        decode_stored,
        decode_weight,
        cotangent,
        decode_factor,
        decode_blocks,
        3 * mesh_rows,
    )
    from_next = from_behind(decode_returned[:mesh_rows], ("tile", "sub"), -1)
    from_prev = from_behind(decode_returned[2 * mesh_rows :], ("tile", "sub"), 1)
    mesh_grad = decode_returned[mesh_rows : 2 * mesh_rows] + from_next + from_prev
    level_part = exact_sum(fine_members.astype(jnp.float32), mesh_grad)
    level_grad = lax.psum(level_part, "sub")
    summit_grad_part = exact_sum(top_members.astype(jnp.float32), level_grad)
    summit_grad_whole = lax.psum(summit_grad_part, "tile")
    summit_slope = (summit_grad_whole * silu_slope(summit_act)).astype(jnp.bfloat16)
    summit_local = outer_sum(summit_in, summit_slope)
    summit_back = times_transposed(summit_slope, summit_weight).astype(jnp.bfloat16)
    level_total = level_grad + summit_factor * jnp.take(summit_back, owner_coarse, axis=0).astype(
        jnp.float32
    )
    middle_slope = (level_total * silu_slope(middle_act)).astype(jnp.bfloat16)
    middle_local = outer_sum(middle_in, middle_slope)
    middle_back = level_total + times_transposed(middle_slope, middle_weight)
    mesh_total = mesh_grad + middle_factor * jnp.take(middle_back, fine_local, axis=0)
    encode_local, unused_rows = edge_backward(
        grid_wide,
        encode_senders,
        encode_targets,
        encode_stored,
        encode_weight,
        mesh_total,
        encode_factor,
        encode_blocks,
        0,
    )
    sub_share = 1.0 / subs
    encode_grad, decode_grad, middle_grad = lax.psum(
        (encode_local, decode_local, sub_share * middle_local), ("tile", "sub")
    )
    return (grid_update, encode_grad, decode_grad, middle_grad, summit_local)


def solution(mesh):
    placed = (
        P(("tile", "sub"), None),
        P(("tile", "sub"), None),
        P(("tile", "sub"), None),
        P(("tile", "sub"), None),
        P(("tile", "sub")),
        P(("tile", "sub")),
        P(("tile", "sub")),
        P(("tile", "sub")),
        P(("tile", "sub")),
        P("tile"),
        P(),
        P(),
        P(),
        P(),
        P(("tile", "sub"), None),
    )
    return jax.shard_map(
        shards,
        mesh=mesh,
        in_specs=placed,
        out_specs=(P(("tile", "sub"), None), P(), P(), P(), P()),
        check_vma=False,
    )
```

profile of v0, /device:TPU:0, one launch (start us, length us, event | category | flops | bytes accessed | tf_op | source)
XLA Modules:
  0.0 564.3 jit_solution(5614955575473783883)
XLA Ops:
  7.2 2.5 collective-permute-start
  15.4 1.6 broadcast_in_dim.93
  17.0 16.3 %while.46 = (s32[]{:T(128)}, f32[128,512]{1,0:T(8,128)S(1)}, f32[1024,512]{1,0:T(8,128)}, s32[]{:T(128)}, s32[1024]{0:T(1024)S(1)}, /*index=5*/s32[1024]{0:T(102...) while((s32[]{:T(128)}, f32[128,512]{1,0:T(8,128)S(1)}, ...), condition=%wide.region_3.5_spmd, body=%wide.region_2.0_spmd.sunk | while | flops 168314624 | bytes 2367415 | solution.py:86
  18.6 1.9 constant_dynamic-update-slice_fusion.7
  22.5 1.9 constant_dynamic-update-slice_fusion.7
  26.5 1.9 constant_dynamic-update-slice_fusion.7
  30.4 1.9 constant_dynamic-update-slice_fusion.7
  34.4 52.0 %all-reduce.7.cloned.1.call-done = f32[128,512]{1,0:T(8,128)} async-done(((f32[128,512]{1,0:T(8,128)}), f32[128,512]{1,0:T(8,128)}) %all-reduce.7.cloned.1.call-update) | async-done | bytes 262160 | tf_op jit(solution)/shard_map/psum | solution.py:159
  86.4 2.0 add_convert_fusion.2
  91.9 76.8 %all-reduce.9.cloned.1.call-done = f32[512,512]{1,0:T(8,128)} async-done(((f32[512,512]{1,0:T(8,128)}), f32[512,512]{1,0:T(8,128)}) %all-reduce.9.cloned.1.call-update) | async-done | bytes 1048592 | tf_op jit(solution)/shard_map/psum | solution.py:165
  168.7 2.7 multiply_convert_fusion.6
  172.4 1.7 collective-permute-start.2
  176.7 2.0 collective-permute-done.3
  179.6 19.5 %while.47 = (s32[]{:T(128)}, f32[128,512]{1,0:T(8,128)}, f32[512,512]{1,0:T(8,128)S(1)}, s32[]{:T(128)}, s32[512]{0:T(512)}, /*index=5*/s32[512]{0:T(512)}, bf16...) while((s32[]{:T(128)}, f32[128,512]{1,0:T(8,128)}, ...), condition=%wide.region_7.10_spmd, body=%wide.region_6.9_spmd.sunk | while | flops 168314624 | bytes 2367799 | solution.py:86
  183.9 2.0 convolution_add_fusion.14
  190.1 2.0 convolution_add_fusion.14
  196.4 2.0 convolution_add_fusion.14
  200.3 22.2 %while.48 = (s32[]{:T(128)}, f32[512,512]{1,0:T(8,128)S(1)}, f32[384,512]{1,0:T(8,128)S(1)}, s32[]{:T(128)}, s32[512]{0:T(512)}, /*index=5*/bf16[384,512]{1,0:T(...) while((s32[]{:T(128)}, f32[512,512]{1,0:T(8,128)S(1)}, ...), condition=%wide.region_9.12_spmd, body=%wide.region_8.11_spmd.sunk | while | flops 438357888 | bytes 8272603 | solution.py:111
  204.1 1.5 convolution_add_fusion.15
  218.4 1.5 convolution_add_fusion.15
  223.9 6.1 %collective-permute-start.5 = (f32[128,512]{1,0:T(8,128)S(1)}, f32[128,512]{1,0:T(8,128)S(1)}, u32[]{:S(2)}, u32[]{:S(2)}) collective-permute-start(f32[128,512]{1,0:T(8,128)S(1)} %get-tuple-element.310), channel_id=1, source_target_pairs={{0,1},{1,2},{2,3},{3,4},{4,5},{5,6},{6,7},{7,8},{8,9},{9,10},{10,1... | collective-permute-start | bytes 786440 | tf_op jit(solution)/shard_map/ppermute | solution.py:26
  231.1 1.6 fusion.48
  232.8 53.1 %all-reduce.11.cloned.1.call-done = f32[128,512]{1,0:T(8,128)} async-done(((f32[128,512]{1,0:T(8,128)}), f32[128,512]{1,0:T(8,128)}) %all-reduce.11.cloned.1.call-update) | async-done | bytes 262160 | tf_op jit(solution)/shard_map/psum | solution.py:205
  285.9 2.5 fusion.42
  288.5 79.6 %all-reduce.13.cloned.1.call-done = f32[512,512]{1,0:T(8,128)} async-done(((f32[512,512]{1,0:T(8,128)}), f32[512,512]{1,0:T(8,128)}) %all-reduce.13.cloned.1.call-update) | async-done | bytes 1048592 | tf_op jit(solution)/shard_map/psum | solution.py:207
  368.1 1.9 multiply_convert_fusion.5
  371.4 1.6 convolution_add_fusion.7
  375.1 18.6 %while.49 = (s32[]{:T(128)}, f32[512,512]{1,0:T(8,128)S(1)}, s32[]{:T(128)}, s32[1024]{0:T(1024)}, bf16[384,512]{1,0:T(8,128)(2,1)S(1)}, /*index=5*/s32[1024]{0:...) while((s32[]{:T(128)}, f32[512,512]{1,0:T(8,128)S(1)}, ...), condition=%wide.region_13.16_spmd, body=%wide.region_12.15_spmd.sunk | while | flops 68161032 | bytes 3551915 | solution.py:111
  393.7 2.8 convolution_multiply_fusion
  398.2 2.7 fusion.44
  400.9 152.5 %all-reduce.15.cloned.1.call-done = (f32[512,512]{1,0:T(8,128)}, f32[512,512]{1,0:T(8,128)}, f32[512,512]{1,0:T(8,128)}) async-done(((f32[512,512]{1,0:T(8,128)}, f32[512,512]{1,0:T(8,128)}, f32[512,512]{1,0:T(8,128)}), (f32[512,512]{1,0:T(8,128)}, f32[512,512]{1,0:T(8,128)}, f32[512,512]{1,0:T(8,128)})) %all-reduce.15.cloned.1.call-update) | async-done | bytes 3145744 | tf_op jit(solution)/shard_map/psum | solution.py:230
  553.4 2.4 copy.68
  (195 shorter events, 73.4 us)
Async XLA Ops:
  7.2 161.6 %copy-start = (bf16[512,512]{1,0:T(8,128)(2,1)S(1)}, bf16[512,512]{1,0:T(8,128)(2,1)}, u32[]{:S(2)}) copy-start(bf16[512,512]{1,0:T(8,128)(2,1)} %param.40) | copy-start | bytes 1572868
  7.2 9.8 %copy-start.5 = (bf16[512,512]{1,0:T(8,128)(2,1)S(1)}, bf16[512,512]{1,0:T(8,128)(2,1)}, u32[]{:S(2)}) copy-start(bf16[512,512]{1,0:T(8,128)(2,1)} %param.37) | copy-start | bytes 1572868
  7.2 79.2 %all-reduce.7.cloned.1.call-start = ((), (), s32[]{:S(2)}) async-start(), calls=%async_computation | async-start | bytes 524288 | tf_op jit(solution)/shard_map/psum | solution.py:159
  7.2 6.5 %collective-permute-start = (bf16[128,512]{1,0:T(8,128)(2,1)}, bf16[128,512]{1,0:T(8,128)(2,1)S(1)}, u32[]{:S(2)}, u32[]{:S(2)}) collective-permute-start(bf16[128,512]{1,0:T(8,128)(2,1)} %param.27), channel_id=1, source_target_pairs={{0,1},{1,2},{2,3},{3,4},{4,5},{5,6},{6,7},{7,8},{8,9},{9,10},{10,1... | collective-permute-start | bytes 393224 | tf_op jit(solution)/shard_map/ppermute | solution.py:17
  9.8 5.6 collective-permute-start.1
  12.5 78.5 %copy-start.21 = (s32[128]{0:T(128)}, s32[128]{0:T(128)S(1)}, u32[]{:S(2)}) copy-start(s32[128]{0:T(128)S(1)} %get-tuple-element.300) | copy-start | bytes 1540
  17.0 16.4 %copy-start.14 = (bf16[128,512]{1,0:T(8,128)(2,1)S(1)}, bf16[128,512]{1,0:T(8,128)(2,1)}, u32[]{:S(2)}) copy-start(bf16[128,512]{1,0:T(8,128)(2,1)} %param.28) | copy-start | bytes 393220
  17.0 69.3 %copy-start.26 = (bf16[512,512]{1,0:T(8,128)(2,1)S(1)}, bf16[512,512]{1,0:T(8,128)(2,1)}, u32[]{:S(2)}) copy-start(bf16[512,512]{1,0:T(8,128)(2,1)} %param.39) | copy-start | bytes 1572868
  33.3 56.3 %copy-start.18 = (s32[1024]{0:T(1024)}, s32[1024]{0:T(1024)S(1)}, u32[]{:S(2)}) copy-start(s32[1024]{0:T(1024)S(1)} %get-tuple-element.780) | copy-start | bytes 12292
  33.4 56.3 %copy-start.19 = (s32[1024]{0:T(1024)}, s32[1024]{0:T(1024)S(1)}, u32[]{:S(2)}) copy-start(s32[1024]{0:T(1024)S(1)} %get-tuple-element.781) | copy-start | bytes 12292
  33.4 55.0 %copy-start.1 = (s32[128]{0:T(128)S(1)}, s32[128]{0:T(128)}, u32[]{:S(2)}) copy-start(s32[128]{0:T(128)} %param.36) | copy-start | bytes 1540
  34.3 134.4 %all-reduce.9.cloned.1.call-start = ((), (), s32[]{:S(2)}) async-start(), calls=%async_computation.1 | async-start | bytes 2097152 | tf_op jit(solution)/shard_map/psum | solution.py:165
  89.7 196.2 %all-reduce.11.cloned.1.call-start = ((), (), s32[]{:S(2)}) async-start(), calls=%async_computation.2 | async-start | bytes 524288 | tf_op jit(solution)/shard_map/psum | solution.py:205
  91.0 81.3 %copy-start.23 = (pred[128]{0:T(512)(128)(4,1)}, pred[128]{0:T(512)(128)(4,1)S(1)}, u32[]{:S(2)}) copy-start(pred[128]{0:T(512)(128)(4,1)S(1)} %get-tuple-element.298) | copy-start | bytes 388
  91.9 83.6 %copy-start.20 = (s32[512]{0:T(512)S(1)}, s32[512]{0:T(512)}, u32[]{:S(2)}) copy-start(s32[512]{0:T(512)} %param.34) | copy-start | bytes 6148
  91.9 83.6 %copy-start.25 = (s32[512]{0:T(512)S(1)}, s32[512]{0:T(512)}, u32[]{:S(2)}) copy-start(s32[512]{0:T(512)} %param.33) | copy-start | bytes 6148
  171.4 8.2 %copy-start.6 = (bf16[512,512]{1,0:T(8,128)(2,1)S(1)}, bf16[512,512]{1,0:T(8,128)(2,1)}, u32[]{:S(2)}) copy-start(bf16[512,512]{1,0:T(8,128)(2,1)} %param.38) | copy-start | bytes 1572868
  172.4 4.2 collective-permute-start.2
  174.1 4.6 collective-permute-start.3
  179.6 20.7 %copy-start.2 = (bf16[128,512]{1,0:T(8,128)(2,1)S(1)}, bf16[128,512]{1,0:T(8,128)(2,1)}, u32[]{:S(2)}) copy-start(bf16[128,512]{1,0:T(8,128)(2,1)} %param.41) | copy-start | bytes 393220
  222.5 65.9 %copy-start.3 = (f32[512,512]{1,0:T(8,128)}, f32[512,512]{1,0:T(8,128)S(1)}, u32[]{:S(2)}) copy-start(f32[512,512]{1,0:T(8,128)S(1)} %get-tuple-element.208) | copy-start | bytes 3145732
  222.6 7.4 %collective-permute-start.4 = (f32[128,512]{1,0:T(8,128)S(1)}, f32[128,512]{1,0:T(8,128)S(1)}, u32[]{:S(2)}, u32[]{:S(2)}) collective-permute-start(f32[128,512]{1,0:T(8,128)S(1)} %get-tuple-element.309), channel_id=1, source_target_pairs={{1,0},{2,1},{3,2},{4,3},{5,4},{6,5},{7,6},{8,7},{9,8},{10,9},{11,1... | collective-permute-start | bytes 786440 | tf_op jit(solution)/shard_map/ppermute | solution.py:26
  223.9 7.2 %collective-permute-start.5 = (f32[128,512]{1,0:T(8,128)S(1)}, f32[128,512]{1,0:T(8,128)S(1)}, u32[]{:S(2)}, u32[]{:S(2)}) collective-permute-start(f32[128,512]{1,0:T(8,128)S(1)} %get-tuple-element.310), channel_id=1, source_target_pairs={{0,1},{1,2},{2,3},{3,4},{4,5},{5,6},{6,7},{7,8},{8,9},{9,10},{10,1... | collective-permute-start | bytes 786440 | tf_op jit(solution)/shard_map/ppermute | solution.py:26
  231.1 138.9 %copy-start.11 = (f32[128,512]{1,0:T(8,128)}, f32[128,512]{1,0:T(8,128)S(1)}, u32[]{:S(2)}) copy-start(f32[128,512]{1,0:T(8,128)S(1)} %collective-permute-done.5) | copy-start | bytes 786436
  232.7 135.3 %all-reduce.13.cloned.1.call-start = ((), (), s32[]{:S(2)}) async-start(), calls=%async_computation.3 | async-start | bytes 2097152 | tf_op jit(solution)/shard_map/psum | solution.py:207
  288.4 264.9 %all-reduce.15.cloned.1.call-start = ((), (), s32[]{:S(2)}) async-start(), calls=%async_computation.4 | async-start | bytes 6291456 | tf_op jit(solution)/shard_map/psum | solution.py:230
  371.3 2.5 copy-start.16
  371.4 2.5 copy-start.24
  375.1 18.6 %copy-start.15 = (f32[128,512]{1,0:T(8,128)S(1)}, f32[128,512]{1,0:T(8,128)}, u32[]{:S(2)}) copy-start(f32[128,512]{1,0:T(8,128)} %all-reduce.11.cloned.1.call-done) | copy-start | bytes 786436
  375.1 18.6 %copy-start.17 = (bf16[128,512]{1,0:T(8,128)(2,1)S(1)}, bf16[128,512]{1,0:T(8,128)(2,1)}, u32[]{:S(2)}) copy-start(bf16[128,512]{1,0:T(8,128)(2,1)} %copy-done.16) | copy-start | bytes 393220
  393.7 2.8 copy-start.4
  553.4 3.4 copy-start.9
  (8 other events, 12.1 us)
Sparse Core Ops, SparseCore 0:
  34.4 51.8 all-reduce.6
  90.4 78.2 all-reduce.8
  232.9 52.9 all-reduce.10
  289.8 78.2 all-reduce.12
  396.7 156.6 all-reduce.14
where the time goes:
time: 566 us; the launch traced here: 564 us
  waiting for transfers between devices  418 us (74%)
  matrix products  53.6 us (9%)
  local copies, waits for them, and re-layouts  34.9 us (6%)
  other arithmetic  17.7 us (3%)
  starting transfers between devices  14.4 us (3%)
  between operations  14.3 us (3%)
  loops' own time  11.6 us (2%)
    psum x1, waiting for transfers between devices, shards(): lax.psum((encode_local, decode_local, sub_share * middle_local), ('tile',...  152 us
    psum x1, waiting for transfers between devices, shards(): summit_grad_whole = lax.psum(summit_grad_part, 'tile')  79.6 us
    psum x1, waiting for transfers between devices, shards(): summit_whole = lax.psum(summit_part, 'tile')  76.8 us
    psum x1, waiting for transfers between devices, shards(): level_grad = lax.psum(level_part, 'sub')  53.1 us
    psum x1, waiting for transfers between devices, shards(): middle_sum = lax.psum(middle_part, 'sub')  52 us
    dot_general x9, matrix products, outer_sum(): lax.dot_general(left, right, (((0,), (0,)), ((), ())), preferred_element_...  16 us
    dot_general x12, matrix products, exact_sum(): jnp.dot(members, values, precision=lax.Precision.HIGHEST, preferred_eleme...  13.6 us
    gather x14, local copies, waits for them, and re-layouts, block_step(): fetched = jnp.take(sources, picked, axis=0)  11.9 us
  transfers between devices with their start and end apart: 11, of which 8 were waited for; matrix products, arithmetic and copies ran while one was open for 2% of the time, Pallas kernels for 0%

commit v1 on v0

--- a/solution.py
+++ b/solution.py
@@ -227,8 +227,9 @@
         0,
     )
     sub_share = 1.0 / subs
-    encode_grad, decode_grad, middle_grad = lax.psum(
-        (encode_local, decode_local, sub_share * middle_local), ("tile", "sub")
+    fit_seats_all = lambda w_in: jax.lax.psum(jax.lax.psum(w_in, "sub"), axis_name="tile")
+    encode_grad, decode_grad, middle_grad = fit_seats_all(
+        (encode_local, decode_local, sub_share * middle_local)
     )
     return (grid_update, encode_grad, decode_grad, middle_grad, summit_local)
 

time: 566 us -> 629 us (1.11)
  waiting for transfers between devices: 418 us -> 482 us
    psum x1 -> x2, waiting for transfers between devices: 152 us -> 217 us  [the longest x1 131 us: shards(): jax.lax.psum(jax.lax.psum(w_in, 'sub'), axis_name='tile')]
  transfers between devices with their start and end apart: 11 -> 12, of which waited for: 8 -> 9; matrix products, arithmetic and copies ran while one was open for 2% -> 1% of each run, Pallas kernels for 0% -> 0%
where the time goes in v1:
time: 629 us; the launch traced here: 627 us
  waiting for transfers between devices  482 us (77%)
  matrix products  52.3 us (8%)
  local copies, waits for them, and re-layouts  33.9 us (5%)
  other arithmetic  17.6 us (3%)
  between operations  14.7 us (2%)
  starting transfers between devices  14.4 us (2%)
  loops' own time  12 us (2%)
    psum x1, waiting for transfers between devices, shards(): jax.lax.psum(jax.lax.psum(w_in, 'sub'), axis_name='tile')  131 us
    psum x1, waiting for transfers between devices, shards(): jax.lax.psum(w_in, 'sub')  86.4 us
    psum x1, waiting for transfers between devices, shards(): summit_grad_whole = lax.psum(summit_grad_part, 'tile')  79.6 us
    psum x1, waiting for transfers between devices, shards(): summit_whole = lax.psum(summit_part, 'tile')  76.8 us
    psum x1, waiting for transfers between devices, shards(): level_grad = lax.psum(level_part, 'sub')  53 us
    psum x1, waiting for transfers between devices, shards(): middle_sum = lax.psum(middle_part, 'sub')  52.3 us
    dot_general x9, matrix products, outer_sum(): lax.dot_general(left, right, (((0,), (0,)), ((), ())), preferred_element_...  14.8 us
    dot_general x12, matrix products, exact_sum(): jnp.dot(members, values, precision=lax.Precision.HIGHEST, preferred_eleme...  13.6 us
  transfers between devices with their start and end apart: 12, of which 9 were waited for; matrix products, arithmetic and copies ran while one was open for 1% of the time, Pallas kernels for 0%

profile of v1, /device:TPU:0, one launch (start us, length us, event | category | flops | bytes accessed | tf_op | source)
XLA Modules:
  0.0 627.3 jit_solution(15287925458555477253)
XLA Ops:
  7.2 2.5 collective-permute-start
  15.4 1.6 broadcast_in_dim.93
  17.0 16.6 %while.46 = (s32[]{:T(128)}, f32[128,512]{1,0:T(8,128)S(1)}, f32[1024,512]{1,0:T(8,128)}, s32[]{:T(128)}, s32[1024]{0:T(1024)S(1)}, /*index=5*/s32[1024]{0:T(102...) while((s32[]{:T(128)}, f32[128,512]{1,0:T(8,128)S(1)}, ...), condition=%wide.region_3.5_spmd, body=%wide.region_2.0_spmd.sunk | while | flops 168314624 | bytes 2367415 | solution.py:86
  18.7 1.9 constant_dynamic-update-slice_fusion.7
  22.6 1.9 constant_dynamic-update-slice_fusion.7
  26.6 1.9 constant_dynamic-update-slice_fusion.7
  30.6 1.9 constant_dynamic-update-slice_fusion.7
  34.6 52.3 %all-reduce.9.cloned.1.call-done = f32[128,512]{1,0:T(8,128)} async-done(((f32[128,512]{1,0:T(8,128)}), f32[128,512]{1,0:T(8,128)}) %all-reduce.9.cloned.1.call-update) | async-done | bytes 262160 | tf_op jit(solution)/shard_map/psum | solution.py:159
  86.9 2.0 add_convert_fusion.2
  92.4 76.8 %all-reduce.11.cloned.1.call-done = f32[512,512]{1,0:T(8,128)} async-done(((f32[512,512]{1,0:T(8,128)}), f32[512,512]{1,0:T(8,128)}) %all-reduce.11.cloned.1.call-update) | async-done | bytes 1048592 | tf_op jit(solution)/shard_map/psum | solution.py:165
  169.3 2.7 multiply_convert_fusion.6
  173.0 1.7 collective-permute-start.2
  177.2 2.0 collective-permute-done.3
  180.1 19.3 %while.47 = (s32[]{:T(128)}, f32[128,512]{1,0:T(8,128)}, f32[512,512]{1,0:T(8,128)S(1)}, s32[]{:T(128)}, s32[512]{0:T(512)}, /*index=5*/s32[512]{0:T(512)}, bf16...) while((s32[]{:T(128)}, f32[128,512]{1,0:T(8,128)}, ...), condition=%wide.region_7.10_spmd, body=%wide.region_6.9_spmd.sunk | while | flops 168314624 | bytes 2367799 | solution.py:86
  184.4 2.0 convolution_add_fusion.14
  190.6 2.0 convolution_add_fusion.14
  196.8 2.0 convolution_add_fusion.14
  200.6 21.9 %while.48 = (s32[]{:T(128)}, f32[512,512]{1,0:T(8,128)S(1)}, f32[384,512]{1,0:T(8,128)S(1)}, s32[]{:T(128)}, s32[512]{0:T(512)}, /*index=5*/bf16[384,512]{1,0:T(...) while((s32[]{:T(128)}, f32[512,512]{1,0:T(8,128)S(1)}, ...), condition=%wide.region_9.12_spmd, body=%wide.region_8.11_spmd.sunk | while | flops 438357888 | bytes 8272603 | solution.py:111
  211.4 1.5 convolution_add_fusion.15
  218.5 1.5 convolution_add_fusion.15
  223.9 6.1 collective-permute-start.5
  231.2 1.6 fusion.48
  232.9 53.0 %all-reduce.13.cloned.1.call-done = f32[128,512]{1,0:T(8,128)} async-done(((f32[128,512]{1,0:T(8,128)}), f32[128,512]{1,0:T(8,128)}) %all-reduce.13.cloned.1.call-update) | async-done | bytes 262160 | tf_op jit(solution)/shard_map/psum | solution.py:205
  285.8 2.5 fusion.42
  288.5 79.6 %all-reduce.15.cloned.1.call-done = f32[512,512]{1,0:T(8,128)} async-done(((f32[512,512]{1,0:T(8,128)}), f32[512,512]{1,0:T(8,128)}) %all-reduce.15.cloned.1.call-update) | async-done | bytes 1048592 | tf_op jit(solution)/shard_map/psum | solution.py:207
  368.0 1.9 multiply_convert_fusion.5
  371.3 1.6 convolution_add_fusion.7
  375.1 18.9 %while.49 = (s32[]{:T(128)}, f32[512,512]{1,0:T(8,128)S(1)}, s32[]{:T(128)}, s32[1024]{0:T(1024)}, bf16[384,512]{1,0:T(8,128)(2,1)S(1)}, /*index=5*/s32[1024]{0:...) while((s32[]{:T(128)}, f32[512,512]{1,0:T(8,128)S(1)}, ...), condition=%wide.region_13.16_spmd, body=%wide.region_12.15_spmd.sunk | while | flops 68161032 | bytes 3551915 | solution.py:111
  394.0 2.8 convolution_multiply_fusion
  396.9 86.4 %all-reduce.19.cloned.1.call-done = (f32[512,512]{1,0:T(8,128)}, f32[512,512]{1,0:T(8,128)}, f32[512,512]{1,0:T(8,128)}) async-done(((f32[512,512]{1,0:T(8,128)}, f32[512,512]{1,0:T(8,128)}, f32[512,512]{1,0:T(8,128)}), (f32[512,512]{1,0:T(8,128)}, f32[512,512]{1,0:T(8,128)}, f32[512,512]{1,0:T(8,128)})) %all-reduce.19.cloned.1.call-update) | async-done | bytes 3145744 | tf_op jit(solution)/shard_map/psum | solution.py:230
  485.5 130.6 %all-reduce.17.cloned.1.call-done = (f32[512,512]{1,0:T(8,128)}, f32[512,512]{1,0:T(8,128)}, f32[512,512]{1,0:T(8,128)}) async-done(((f32[512,512]{1,0:T(8,128)}, f32[512,512]{1,0:T(8,128)}, f32[512,512]{1,0:T(8,128)}), (f32[512,512]{1,0:T(8,128)}, f32[512,512]{1,0:T(8,128)}, f32[512,512]{1,0:T(8,128)})) %all-reduce.17.cloned.1.call-update) | async-done | bytes 3145744 | tf_op jit(solution)/shard_map/psum | solution.py:230
  616.1 2.4 copy.71
  (200 shorter events, 73.9 us)
Async XLA Ops:
  7.2 162.1 %copy-start = (bf16[512,512]{1,0:T(8,128)(2,1)S(1)}, bf16[512,512]{1,0:T(8,128)(2,1)}, u32[]{:S(2)}) copy-start(bf16[512,512]{1,0:T(8,128)(2,1)} %param.40) | copy-start | bytes 1572868
  7.2 9.8 %copy-start.5 = (bf16[512,512]{1,0:T(8,128)(2,1)S(1)}, bf16[512,512]{1,0:T(8,128)(2,1)}, u32[]{:S(2)}) copy-start(bf16[512,512]{1,0:T(8,128)(2,1)} %param.37) | copy-start | bytes 1572868
  7.2 79.7 %all-reduce.9.cloned.1.call-start = ((), (), s32[]{:S(2)}) async-start(), calls=%async_computation | async-start | bytes 524288 | tf_op jit(solution)/shard_map/psum | solution.py:159
  7.2 6.6 %collective-permute-start = (bf16[128,512]{1,0:T(8,128)(2,1)}, bf16[128,512]{1,0:T(8,128)(2,1)S(1)}, u32[]{:S(2)}, u32[]{:S(2)}) collective-permute-start(bf16[128,512]{1,0:T(8,128)(2,1)} %param.27), channel_id=1, source_target_pairs={{0,1},{1,2},{2,3},{3,4},{4,5},{5,6},{6,7},{7,8},{8,9},{9,10},{10,1... | collective-permute-start | bytes 393224 | tf_op jit(solution)/shard_map/ppermute | solution.py:17
  9.8 5.6 collective-permute-start.1
  12.5 79.1 %copy-start.22 = (s32[128]{0:T(128)}, s32[128]{0:T(128)S(1)}, u32[]{:S(2)}) copy-start(s32[128]{0:T(128)S(1)} %get-tuple-element.303) | copy-start | bytes 1540
  17.0 16.6 %copy-start.15 = (bf16[128,512]{1,0:T(8,128)(2,1)S(1)}, bf16[128,512]{1,0:T(8,128)(2,1)}, u32[]{:S(2)}) copy-start(bf16[128,512]{1,0:T(8,128)(2,1)} %param.28) | copy-start | bytes 393220
  17.0 69.9 %copy-start.27 = (bf16[512,512]{1,0:T(8,128)(2,1)S(1)}, bf16[512,512]{1,0:T(8,128)(2,1)}, u32[]{:S(2)}) copy-start(bf16[512,512]{1,0:T(8,128)(2,1)} %param.39) | copy-start | bytes 1572868
  33.6 56.6 %copy-start.19 = (s32[1024]{0:T(1024)}, s32[1024]{0:T(1024)S(1)}, u32[]{:S(2)}) copy-start(s32[1024]{0:T(1024)S(1)} %get-tuple-element.797) | copy-start | bytes 12292
  33.6 56.6 %copy-start.20 = (s32[1024]{0:T(1024)}, s32[1024]{0:T(1024)S(1)}, u32[]{:S(2)}) copy-start(s32[1024]{0:T(1024)S(1)} %get-tuple-element.798) | copy-start | bytes 12292
  33.6 55.3 %copy-start.1 = (s32[128]{0:T(128)S(1)}, s32[128]{0:T(128)}, u32[]{:S(2)}) copy-start(s32[128]{0:T(128)} %param.36) | copy-start | bytes 1540
  34.6 134.7 %all-reduce.11.cloned.1.call-start = ((), (), s32[]{:S(2)}) async-start(), calls=%async_computation.1 | async-start | bytes 2097152 | tf_op jit(solution)/shard_map/psum | solution.py:165
  90.2 195.6 %all-reduce.13.cloned.1.call-start = ((), (), s32[]{:S(2)}) async-start(), calls=%async_computation.2 | async-start | bytes 524288 | tf_op jit(solution)/shard_map/psum | solution.py:205
  90.3 79.0 %copy-start.23 = (s32[1024]{0:T(1024)}, s32[1024]{0:T(1024)S(1)}, u32[]{:S(2)}) copy-start(s32[1024]{0:T(1024)S(1)} %pad_clamp_fusion.8) | copy-start | bytes 12292
  91.5 81.3 %copy-start.24 = (pred[128]{0:T(512)(128)(4,1)}, pred[128]{0:T(512)(128)(4,1)S(1)}, u32[]{:S(2)}) copy-start(pred[128]{0:T(512)(128)(4,1)S(1)} %get-tuple-element.301) | copy-start | bytes 388
  92.4 83.5 %copy-start.21 = (s32[512]{0:T(512)S(1)}, s32[512]{0:T(512)}, u32[]{:S(2)}) copy-start(s32[512]{0:T(512)} %param.34) | copy-start | bytes 6148
  92.4 83.5 %copy-start.26 = (s32[512]{0:T(512)S(1)}, s32[512]{0:T(512)}, u32[]{:S(2)}) copy-start(s32[512]{0:T(512)} %param.33) | copy-start | bytes 6148
  173.0 4.3 collective-permute-start.2
  174.6 4.6 collective-permute-start.3
  180.1 20.5 %copy-start.2 = (bf16[128,512]{1,0:T(8,128)(2,1)S(1)}, bf16[128,512]{1,0:T(8,128)(2,1)}, u32[]{:S(2)}) copy-start(bf16[128,512]{1,0:T(8,128)(2,1)} %param.41) | copy-start | bytes 393220
  222.6 65.8 %copy-start.3 = (f32[512,512]{1,0:T(8,128)}, f32[512,512]{1,0:T(8,128)S(1)}, u32[]{:S(2)}) copy-start(f32[512,512]{1,0:T(8,128)S(1)} %get-tuple-element.208) | copy-start | bytes 3145732
  222.6 7.4 %collective-permute-start.4 = (f32[128,512]{1,0:T(8,128)S(1)}, f32[128,512]{1,0:T(8,128)S(1)}, u32[]{:S(2)}, u32[]{:S(2)}) collective-permute-start(f32[128,512]{1,0:T(8,128)S(1)} %get-tuple-element.312), channel_id=1, source_target_pairs={{1,0},{2,1},{3,2},{4,3},{5,4},{6,5},{7,6},{8,7},{9,8},{10,9},{11,1... | collective-permute-start | bytes 786440 | tf_op jit(solution)/shard_map/ppermute | solution.py:26
  223.9 7.2 %collective-permute-start.5 = (f32[128,512]{1,0:T(8,128)S(1)}, f32[128,512]{1,0:T(8,128)S(1)}, u32[]{:S(2)}, u32[]{:S(2)}) collective-permute-start(f32[128,512]{1,0:T(8,128)S(1)} %get-tuple-element.313), channel_id=1, source_target_pairs={{0,1},{1,2},{2,3},{3,4},{4,5},{5,6},{6,7},{7,8},{8,9},{9,10},{10,1... | collective-permute-start | bytes 786440 | tf_op jit(solution)/shard_map/ppermute | solution.py:26
  231.2 138.8 %copy-start.12 = (f32[128,512]{1,0:T(8,128)}, f32[128,512]{1,0:T(8,128)S(1)}, u32[]{:S(2)}) copy-start(f32[128,512]{1,0:T(8,128)S(1)} %collective-permute-done.5) | copy-start | bytes 786436
  232.8 135.2 %all-reduce.15.cloned.1.call-start = ((), (), s32[]{:S(2)}) async-start(), calls=%async_computation.3 | async-start | bytes 2097152 | tf_op jit(solution)/shard_map/psum | solution.py:207
  288.4 194.9 %all-reduce.19.cloned.1.call-start = ((), (), s32[]{:S(2)}) async-start(), calls=%async_computation.5 | async-start | bytes 6291456 | tf_op jit(solution)/shard_map/psum | solution.py:230
  375.0 18.9 %copy-start.16 = (f32[128,512]{1,0:T(8,128)S(1)}, f32[128,512]{1,0:T(8,128)}, u32[]{:S(2)}) copy-start(f32[128,512]{1,0:T(8,128)} %all-reduce.13.cloned.1.call-done) | copy-start | bytes 786436
  375.1 18.9 %copy-start.18 = (bf16[128,512]{1,0:T(8,128)(2,1)S(1)}, bf16[128,512]{1,0:T(8,128)(2,1)}, u32[]{:S(2)}) copy-start(bf16[128,512]{1,0:T(8,128)(2,1)} %copy-done.17) | copy-start | bytes 393220
  396.9 86.5 %copy-start.13 = (f32[128,512]{1,0:T(8,128)S(1)}, f32[128,512]{1,0:T(8,128)}, u32[]{:S(2)}) copy-start(f32[128,512]{1,0:T(8,128)} %get-tuple-element.203) | copy-start | bytes 786436
  396.9 86.5 %copy-start.14 = (bf16[128,512]{1,0:T(8,128)(2,1)S(1)}, bf16[128,512]{1,0:T(8,128)(2,1)}, u32[]{:S(2)}) copy-start(bf16[128,512]{1,0:T(8,128)(2,1)} %param.27) | copy-start | bytes 393220
  396.9 87.2 %copy-start.9 = (f32[512,512]{1,0:T(8,128)S(1)}, f32[512,512]{1,0:T(8,128)}, u32[]{:S(2)}) copy-start(f32[512,512]{1,0:T(8,128)} %all-reduce.11.cloned.1.call-done) | copy-start | bytes 3145732
  396.9 219.2 %all-reduce.17.cloned.1.call-start = ((), (), s32[]{:S(2)}) async-start(), calls=%async_computation.4 | async-start | bytes 6291456 | tf_op jit(solution)/shard_map/psum | solution.py:230
  (10 other events, 27.5 us)
Sparse Core Ops, SparseCore 0:
  34.7 52.1 all-reduce.8
  91.0 78.1 all-reduce.10
  232.9 52.8 all-reduce.12
  289.8 78.2 all-reduce.14
  397.0 86.2 all-reduce.18
  487.1 128.9 all-reduce.16
